TPU v7x, 256 devices: a whole 4x4x8 slice. The times are simulated.
256 devices in a mesh: dp: 64 (over x, z, core), mp: 4 (over y).
Axes of the slice: x: 4, y: 4, z: 8, core: 2. Of those that a mesh axis runs over, the one named last changes fastest.
Arguments:
- features: bfloat16 [16384, 512], P('dp'), may hold values from -6 to 6
- adjacency: bfloat16 [4096, 4, 128, 128], P('dp'), may hold values from -0.125 to 0.125
- source_block: int32 [4096, 4], P('dp'), may hold values from 0 to 1
- edge_type: int32 [4096, 4], P('dp'), may hold values from 0 to 19
- target_block: int32 [4096, 4], P('dp'), may hold values from 0 to 1
- live_count: int32 [64, 64], P('dp'), may hold values from 3 to 4, as said below
- relation_weight: bfloat16 [20, 512, 512], P(None, None, 'mp'), may hold values from -0.25 to 0.25
- self_weight: bfloat16 [512, 512], P(None, 'mp'), may hold values from -0.25 to 0.25
- layer_bias: bfloat16 [512], P('mp'), may hold values from -3 to 3
- norm_gain: bfloat16 [512], replicated, may hold values from 0.5 to 1.5
Outputs:
- node_states: bfloat16 [16384, 512], P(('dp', 'mp'))
Inputs may be any that keep to these rules, and one draw needn't show every extreme that they name: `source_block`: row s * 64 + d names a block among sender s's 2 blocks. `target_block`: row d * 64 + s names a block among receiver d's 2 blocks. live_count[d, s] live slots from sender s to receiver d, the first ones; some receiver has all 4 slots live from every sender.
All inputs are finite; a program needn't handle non-finite values.
Results may differ from a plain program's by a relative error of at most 0.007.
Values may be sent and summed in bfloat16 or wider, within the bound.
A program may use at most 128 MiB of HBM per device.

v0:
```python
import jax
import jax.numpy as jnp
from jax import lax
from jax.sharding import PartitionSpec as P

BLK = 128
epsilon = 1e-05


def sent_together(arrays, axis, split_dim, concat_dim, along):
    widths = [a.shape[along] for a in arrays]
    both = jnp.concatenate(arrays, axis=along)
    filled = lax.all_to_all(both, axis, split_axis=split_dim, concat_axis=concat_dim, tiled=True)
    return tuple(jnp.split(filled, [sum(widths[:k]) for k in range(1, len(widths))], axis=along))


def split_up(shard, dim, peers):
    dims = shard.shape
    tiles = shard.reshape(*dims[:dim], peers, dims[dim] // peers, *dims[dim + 1 :])
    return jnp.moveaxis(tiles, dim, 0)


def summed_on_arrival(shard, axis, dim):
    peers = lax.axis_size(axis)
    tiles = lax.all_to_all(split_up(shard, dim, peers), axis, 0, 0, tiled=True)
    return jnp.sum(tiles.astype(jnp.float32), axis=0)


def block_table(features, relation_weight, blocks):
    stacked = features.reshape(blocks, BLK, features.shape[1])
    lookup = jnp.einsum(
        "bid,rdc->bric", stacked, relation_weight, preferred_element_type=jnp.float32
    )
    return lookup.astype(jnp.bfloat16).reshape(
        blocks * relation_weight.shape[0], BLK, relation_weight.shape[2]
    )


def transform_slots(lookup, lookup_rows, adj_tiles):
    chosen = jnp.take(lookup, lookup_rows, axis=0)
    return jnp.einsum("nij,njc->nic", adj_tiles, chosen, preferred_element_type=jnp.float32)


def selector(targets, counts, blocks):
    slot_count = targets.shape[1]
    active = jnp.arange(slot_count, dtype=jnp.int32)[None, :] < counts[:, None]
    matches = targets[:, :, None] == jnp.arange(blocks, dtype=jnp.int32)[None, None, :]
    return jnp.logical_and(matches, active[:, :, None]).astype(jnp.float32)


def per_device(
    features,
    adjacency,
    source_block,
    edge_type,
    target_block,
    live_count,
    relation_weight,
    self_weight,
    layer_bias,
    norm_gain,
):
    peer_count = lax.axis_size("dp")
    slot_count = source_block.shape[1]
    node_rows = features.shape[0]
    blocks = node_rows // BLK
    columns = relation_weight.shape[2]
    lookup = block_table(features, relation_weight, blocks)
    lookup_rows = (source_block * relation_weight.shape[0] + edge_type).reshape(
        peer_count * slot_count
    )
    flat_tiles = adjacency.reshape(peer_count * slot_count, BLK, BLK)
    routed, routed_count = sent_together(
        (target_block, live_count.reshape(peer_count, 1)), "dp", 0, 0, 1
    )
    weights = selector(routed, routed_count[:, 0], blocks)
    receivers = node_rows * lax.axis_size("dp") // node_rows
    message = transform_slots(lookup, lookup_rows, flat_tiles).reshape(
        receivers, slot_count, BLK * columns
    )
    summed = jnp.einsum("rkb,rkx->rbx", weights, message, precision=lax.Precision.HIGHEST)
    aggregate = summed_on_arrival(
        summed.reshape(receivers * blocks * BLK, columns).astype(jnp.bfloat16), "dp", 0
    )
    own_term = jnp.dot(features, self_weight, preferred_element_type=jnp.float32)
    hidden = jax.nn.relu(own_term + aggregate + layer_bias.astype(jnp.float32)).astype(jnp.bfloat16)
    by_rows = lax.all_to_all(hidden, "mp", split_axis=0, concat_axis=1, tiled=True)
    values = by_rows.astype(jnp.float32)
    inverse_rms = lax.rsqrt(jnp.mean(values * values, axis=1, keepdims=True) + epsilon)
    return (values * inverse_rms * norm_gain.astype(jnp.float32)).astype(jnp.bfloat16)


def solution(mesh):
    return jax.shard_map(
        per_device,
        mesh=mesh,
        in_specs=(
            P("dp", None),
            P("dp", None, None, None),
            P("dp", None),
            P("dp", None),
            P("dp", None),
            P("dp", None),
            P(None, None, "mp"),
            P(None, "mp"),
            P("mp"),
            P(),
        ),
        out_specs=P(("dp", "mp"), None),
        check_vma=False,
    )
```

profile of v0, /device:TPU:1, one launch (start us, length us, event | category | flops | bytes accessed | tf_op | source)
XLA Modules:
  0.0 229.2 jit_solution(922433717765947294)
XLA Ops:
  0.0 0.0 copy-start
  0.0 0.9 pad_add_fusion
  0.9 0.7 copy.40
  1.6 13.0 %all-to-all-start = ((s32[64,1,5]{2,1,0:T(1,128)}), s32[64,1,5]{2,1,0:T(1,128)S(1)}, u32[]{:S(2)}, u32[]{:S(2)}) async-start(s32[64,1,5]{2,1,0:T(1,128)} %bitcast.1), calls=%async_computation | async-start | bytes 65536 | tf_op jit(solution)/shard_map/all_to_all | solution.py:13
  14.6 0.7 multiply_add_fusion
  15.3 0.1 copy.41
  15.4 0.1 reshape.102
  15.5 0.1 reshape.99
  15.6 0.0 copy-done
  15.6 2.9 %fusion.8 = bf16[2,20,128,128]{2,3,0,1:T(8,128)(2,1)} fusion(bf16[2,128,512,1]{2,1,0,3:T(8,128)(2,1)} %bitcast.41, bf16[20,512,128]{2,1,0:T(8,128)(2,1)S(1)} %copy-done), kind=kOutput, calls=%fused_computation.10 | convolution fusion | flops 671744000 | bytes 4194304 | tf_op jit(solution)/shard_map/bid,rdc->bric/dot_general | solution.py:31
  18.5 1.8 copy.43
  20.3 8.6 %gather_fusion = bf16[256,128,128]{2,1,0:T(8,128)(2,1)} fusion(bf16[40,128,128]{2,1,0:T(8,128)(2,1)S(1)} %bitcast.39, s32[1024]{0:T(1024)S(1)} %pad_clamp_fusion), kind=kCustom, calls=%fused_computation | custom fusion | bytes 16778240 | tf_op jit(solution)/shard_map/jit(_take)/gather | solution.py:40
  28.9 13.2 %convolution_bitcast_fusion = f32[256,128,128]{1,2,0:T(8,128)} fusion(bf16[256,128,128]{2,1,0:T(8,128)(2,1)} %bitcast.40, bf16[256,128,128]{2,1,0:T(8,128)(2,1)} %gather_fusion, pred[256]{0:T(512)(128)(4,1)S(1)} %compare_and_fusion), kind=kOutput, calls=%fused_computation.2 | convolution fusion | flops 1077936128 | bytes 33554688 | tf_op jit(solution)/shard_map/nij,njc->nic/dot_general | solution.py:41
  42.1 17.5 %copy.46 = f32[256,128,128]{2,1,0:T(8,128)} copy(f32[256,128,128]{1,2,0:T(8,128)} %convolution_bitcast_fusion) | data formatting | bytes 33554432 | tf_op jit(solution)/shard_map/nij,njc->nic/dot_general | solution.py:41
  59.6 20.2 %reshape.104 = f32[64,4,16384]{2,1,0:T(4,128)} reshape(f32[256,128,128]{2,1,0:T(8,128)} %copy.46) | data formatting | bytes 33554432 | tf_op jit(solution)/shard_map/reshape | solution.py:78
  79.8 0.0 all-to-all-done
  79.8 0.2 slice_reduce_fusion
  80.0 0.1 iota_compare_fusion
  80.1 21.4 %convolution_convert_fusion = bf16[64,2,16384]{2,1,0:T(2,128)(2,1)} fusion(f32[64,4,16384]{2,1,0:T(4,128)} %reshape.104, pred[64,4]{1,0:T(8,128)(4,1)S(1)} %iota_compare_fusion, s32[64,4]{1,0:T(8,128)S(1)} %bitcast.43), kind=kOutput, calls=%fused_computation.1 | convolution fusion | flops 102761472 | bytes 20972800 | tf_op jit(solution)/shard_map/rkb,rkx->rbx/dot_general | solution.py:81
  101.5 8.0 %convert_element_type.45 = bf16[64,256,128]{2,1,0:T(8,128)(2,1)} reshape(bf16[64,2,16384]{2,1,0:T(2,128)(2,1)} %convolution_convert_fusion) | data formatting | bytes 8388608 | tf_op jit(solution)/shard_map/convert_element_type | solution.py:83
  109.5 10.7 %all-to-all-start.1 = ((bf16[64,256,128]{2,1,0:T(8,128)(2,1)}), bf16[64,256,128]{2,1,0:T(8,128)(2,1)}, u32[]{:S(2)}, u32[]{:S(2)}) async-start(bf16[64,256,128]{2,1,0:T(8,128)(2,1)} %convert_element_type.45), calls=%async_computation.1 | async-start | bytes 8388608 | tf_op jit(solution)/shard_map/all_to_all | solution.py:25
  120.1 0.0 copy-done.5
  120.2 95.8 %all-to-all-done.1 = bf16[64,256,128]{2,1,0:T(8,128)(2,1)} async-done(((bf16[64,256,128]{2,1,0:T(8,128)(2,1)}), bf16[64,256,128]{2,1,0:T(8,128)(2,1)}, u32[]{:S(2)}, u32[]{:S(2)}) %all-to-all-start.1) | async-done | bytes 4194336 | tf_op jit(solution)/shard_map/all_to_all | solution.py:25
  216.0 2.8 %convert_reduce_fusion = f32[256,128]{1,0:T(8,128)S(1)} fusion(bf16[64,256,128]{2,1,0:T(8,128)(2,1)} %all-to-all-done.1), kind=kLoop, calls=%fused_computation.3 | loop fusion | flops 4161536 | bytes 4325376 | tf_op jit(solution)/shard_map/reduce_sum | solution.py:26
  218.8 0.0 copy-done.2
  218.8 0.0 copy-done.3
  218.8 0.9 fusion.13
  219.7 4.2 %all-to-all-start.2 = ((bf16[4,64,128]{2,1,0:T(8,128)(2,1)}), bf16[4,64,128]{2,1,0:T(8,128)(2,1)S(1)}, u32[]{:S(2)}, u32[]{:S(2)}) async-start(bf16[4,64,128]{2,1,0:T(8,128)(2,1)} %bitcast.11), calls=%async_computation.2 | async-start | bytes 131072 | tf_op jit(solution)/shard_map/all_to_all | solution.py:87
  223.8 0.0 copy-done.4
  223.8 4.5 %all-to-all-done.2 = bf16[4,64,128]{2,1,0:T(8,128)(2,1)S(1)} async-done(((bf16[4,64,128]{2,1,0:T(8,128)(2,1)}), bf16[4,64,128]{2,1,0:T(8,128)(2,1)S(1)}, u32[]{:S(2)}, u32[]{:S(2)}) %all-to-all-start.2) | async-done | bytes 65568 | tf_op jit(solution)/shard_map/all_to_all | solution.py:87
  228.3 0.1 fusion.14
  228.4 0.7 fusion.16
  (12 shorter events, 0.0 us)
Async XLA Ops:
  0.0 15.6 %copy-start = (bf16[20,512,128]{2,1,0:T(8,128)(2,1)S(1)}, bf16[20,512,128]{2,1,0:T(8,128)(2,1)}, u32[]{:S(2)}) copy-start(bf16[20,512,128]{2,1,0:T(8,128)(2,1)} %param.16) | copy-start | bytes 7864324
  1.6 78.2 %all-to-all-start = ((s32[64,1,5]{2,1,0:T(1,128)}), s32[64,1,5]{2,1,0:T(1,128)S(1)}, u32[]{:S(2)}, u32[]{:S(2)}) async-start(s32[64,1,5]{2,1,0:T(1,128)} %bitcast.1), calls=%async_computation | async-start | bytes 65536 | tf_op jit(solution)/shard_map/all_to_all | solution.py:13
  101.5 18.6 %copy-start.5 = (bf16[128]{0:T(256)(128)(2,1)S(1)}, bf16[128]{0:T(256)(128)(2,1)}, u32[]{:S(2)}) copy-start(bf16[128]{0:T(256)(128)(2,1)} %param.18) | copy-start | bytes 772
  101.5 127.7 %copy-start.1 = (bf16[20,512,128]{2,1,0:T(8,128)(2,1)S(1)}, bf16[20,512,128]{2,1,0:T(8,128)(2,1)}, u32[]{:S(2)}) copy-start(bf16[20,512,128]{2,1,0:T(8,128)(2,1)} %param.16) | copy-start | bytes 7864324
  109.5 109.3 %copy-start.2 = (bf16[256,512]{1,0:T(8,128)(2,1)S(1)}, bf16[256,512]{1,0:T(8,128)(2,1)}, u32[]{:S(2)}) copy-start(bf16[256,512]{1,0:T(8,128)(2,1)} %param.10) | copy-start | bytes 786436
  109.5 109.3 %copy-start.3 = (bf16[512,128]{1,0:T(8,128)(2,1)S(1)}, bf16[512,128]{1,0:T(8,128)(2,1)}, u32[]{:S(2)}) copy-start(bf16[512,128]{1,0:T(8,128)(2,1)} %param.17) | copy-start | bytes 393220
  109.5 114.4 %copy-start.4 = (bf16[512]{0:T(512)(128)(2,1)S(1)}, bf16[512]{0:T(512)(128)(2,1)}, u32[]{:S(2)}) copy-start(bf16[512]{0:T(512)(128)(2,1)} %param.19) | copy-start | bytes 3076
  109.5 106.5 %all-to-all-start.1 = ((bf16[64,256,128]{2,1,0:T(8,128)(2,1)}), bf16[64,256,128]{2,1,0:T(8,128)(2,1)}, u32[]{:S(2)}, u32[]{:S(2)}) async-start(bf16[64,256,128]{2,1,0:T(8,128)(2,1)} %convert_element_type.45), calls=%async_computation.1 | async-start | bytes 8388608 | tf_op jit(solution)/shard_map/all_to_all | solution.py:25
  219.7 8.7 %all-to-all-start.2 = ((bf16[4,64,128]{2,1,0:T(8,128)(2,1)}), bf16[4,64,128]{2,1,0:T(8,128)(2,1)S(1)}, u32[]{:S(2)}, u32[]{:S(2)}) async-start(bf16[4,64,128]{2,1,0:T(8,128)(2,1)} %bitcast.11), calls=%async_computation.2 | async-start | bytes 131072 | tf_op jit(solution)/shard_map/all_to_all | solution.py:87
where the time goes:
time: 230 us; the launch traced here: 229 us
  waiting for transfers between devices  100 us (43%)
  local copies, waits for them, and re-layouts  57.3 us (25%)
  matrix products  38.4 us (17%)
  starting transfers between devices  27.8 us (12%)
  other arithmetic  5.3 us (2%)
    all_to_all x1, waiting for transfers between devices, summed_on_arrival(): tiles = lax.all_to_all(split_up(shard, dim, peers), axis, 0, 0, tiled=True)  95.8 us
    dot_general x1, matrix products, per_device(): jnp.einsum('rkb,rkx->rbx', weights, message, precision=lax.Precision.HIGH...  21.4 us
    reshape x1, local copies, waits for them, and re-layouts, per_device(): transform_slots(lookup, lookup_rows, flat_tiles)  20.2 us
    dot_general x1, local copies, waits for them, and re-layouts, transform_slots(): jnp.einsum('nij,njc->nic', adj_tiles, chosen, preferred_element_type=jnp....  17.5 us
    dot_general x1, matrix products, transform_slots(): jnp.einsum('nij,njc->nic', adj_tiles, chosen, preferred_element_type=jnp....  13.2 us
    all_to_all x1, starting transfers between devices, sent_together(): lax.all_to_all(both, axis, split_axis=split_dim, concat_axis=concat_dim,...  13 us
    all_to_all x1, starting transfers between devices, summed_on_arrival(): tiles = lax.all_to_all(split_up(shard, dim, peers), axis, 0, 0, tiled=True)  10.7 us
    gather x1, local copies, waits for them, and re-layouts, transform_slots(): chosen = jnp.take(lookup, lookup_rows, axis=0)  8.61 us
  transfers between devices with their start and end apart: 3, of which 2 were waited for; matrix products, arithmetic and copies ran while one was open for 28% of the time, Pallas kernels for 0%

commit v1 on v0

--- a/solution.py
+++ b/solution.py
@@ -5,6 +5,13 @@
 
 BLK = 128
 epsilon = 1e-05
+
+
+def exchange_blocks(array, axis, split, join):
+    count = lax.axis_size(axis)
+    tiles = jnp.stack(jnp.split(array, count, axis=split), axis=0)
+    tiles = lax.all_to_all(tiles, axis, split_axis=0, concat_axis=0)
+    return jnp.concatenate(tiles, axis=join)
 
 
 def sent_together(arrays, axis, split_dim, concat_dim, along):
@@ -84,7 +91,7 @@
     )
     own_term = jnp.dot(features, self_weight, preferred_element_type=jnp.float32)
     hidden = jax.nn.relu(own_term + aggregate + layer_bias.astype(jnp.float32)).astype(jnp.bfloat16)
-    by_rows = lax.all_to_all(hidden, "mp", split_axis=0, concat_axis=1, tiled=True)
+    by_rows = exchange_blocks(hidden, "mp", 0, 1)
     values = by_rows.astype(jnp.float32)
     inverse_rms = lax.rsqrt(jnp.mean(values * values, axis=1, keepdims=True) + epsilon)
     return (values * inverse_rms * norm_gain.astype(jnp.float32)).astype(jnp.bfloat16)

time: 230 us -> 230 us (level)
  no operation moved by 1% of the time
where the time goes in v1:
time: 230 us; the launch traced here: 229 us
  waiting for transfers between devices  100 us (43%)
  local copies, waits for them, and re-layouts  57.3 us (25%)
  matrix products  37.8 us (16%)
  starting transfers between devices  27.8 us (12%)
  other arithmetic  5.94 us (3%)
    all_to_all x1, waiting for transfers between devices, summed_on_arrival(): tiles = lax.all_to_all(split_up(shard, dim, peers), axis, 0, 0, tiled=True)  95.8 us
    dot_general x1, matrix products, per_device(): jnp.einsum('rkb,rkx->rbx', weights, message, precision=lax.Precision.HIGH...  21.4 us
    reshape x1, local copies, waits for them, and re-layouts, per_device(): transform_slots(lookup, lookup_rows, flat_tiles)  20.2 us
    dot_general x1, local copies, waits for them, and re-layouts, transform_slots(): jnp.einsum('nij,njc->nic', adj_tiles, chosen, preferred_element_type=jnp....  17.5 us
    dot_general x1, matrix products, transform_slots(): jnp.einsum('nij,njc->nic', adj_tiles, chosen, preferred_element_type=jnp....  13.2 us
    all_to_all x1, starting transfers between devices, sent_together(): lax.all_to_all(both, axis, split_axis=split_dim, concat_axis=concat_dim,...  13 us
    all_to_all x1, starting transfers between devices, summed_on_arrival(): tiles = lax.all_to_all(split_up(shard, dim, peers), axis, 0, 0, tiled=True)  10.7 us
    gather x1, local copies, waits for them, and re-layouts, transform_slots(): chosen = jnp.take(lookup, lookup_rows, axis=0)  8.6 us
  transfers between devices with their start and end apart: 3, of which 2 were waited for; matrix products, arithmetic and copies ran while one was open for 28% of the time, Pallas kernels for 0%

profile of v1, /device:TPU:1, one launch (start us, length us, event | category | flops | bytes accessed | tf_op | source)
XLA Modules:
  0.0 229.2 jit_solution(13949549175878680359)
XLA Ops:
  0.0 0.0 copy-start
  0.0 0.9 pad_add_fusion
  0.9 0.7 copy.39
  1.6 13.0 %all-to-all-start = ((s32[64,1,5]{2,1,0:T(1,128)}), s32[64,1,5]{2,1,0:T(1,128)S(1)}, u32[]{:S(2)}, u32[]{:S(2)}) async-start(s32[64,1,5]{2,1,0:T(1,128)} %bitcast.1), calls=%async_computation | async-start | bytes 65536 | tf_op jit(solution)/shard_map/all_to_all | solution.py:20
  14.6 0.7 multiply_add_fusion
  15.3 0.1 copy.40
  15.4 0.1 reshape.101
  15.5 0.1 reshape.98
  15.6 2.9 %fusion.8 = bf16[2,20,128,128]{2,3,0,1:T(8,128)(2,1)} fusion(bf16[2,128,512,1]{2,1,0,3:T(8,128)(2,1)} %bitcast.48, bf16[20,512,128]{2,1,0:T(8,128)(2,1)S(1)} %copy-done), kind=kOutput, calls=%fused_computation.10 | convolution fusion | flops 671744000 | bytes 4194304 | tf_op jit(solution)/shard_map/bid,rdc->bric/dot_general | solution.py:38
  18.5 1.8 copy.42
  20.3 8.6 %gather_fusion = bf16[256,128,128]{2,1,0:T(8,128)(2,1)} fusion(bf16[40,128,128]{2,1,0:T(8,128)(2,1)S(1)} %bitcast.46, s32[1024]{0:T(1024)S(1)} %pad_clamp_fusion), kind=kCustom, calls=%fused_computation | custom fusion | bytes 16778240 | tf_op jit(solution)/shard_map/jit(_take)/gather | solution.py:47
  28.9 13.2 %convolution_bitcast_fusion = f32[256,128,128]{1,2,0:T(8,128)} fusion(bf16[256,128,128]{2,1,0:T(8,128)(2,1)} %bitcast.47, bf16[256,128,128]{2,1,0:T(8,128)(2,1)} %gather_fusion, pred[256]{0:T(512)(128)(4,1)S(1)} %compare_and_fusion), kind=kOutput, calls=%fused_computation.2 | convolution fusion | flops 1077936128 | bytes 33554688 | tf_op jit(solution)/shard_map/nij,njc->nic/dot_general | solution.py:48
  42.1 17.5 %copy.45 = f32[256,128,128]{2,1,0:T(8,128)} copy(f32[256,128,128]{1,2,0:T(8,128)} %convolution_bitcast_fusion) | data formatting | bytes 33554432 | tf_op jit(solution)/shard_map/nij,njc->nic/dot_general | solution.py:48
  59.6 20.2 %reshape.103 = f32[64,4,16384]{2,1,0:T(4,128)} reshape(f32[256,128,128]{2,1,0:T(8,128)} %copy.45) | data formatting | bytes 33554432 | tf_op jit(solution)/shard_map/reshape | solution.py:85
  79.8 0.0 all-to-all-done
  79.8 0.2 slice_reduce_fusion
  80.0 0.1 iota_compare_fusion
  80.1 21.4 %convolution_convert_fusion = bf16[64,2,16384]{2,1,0:T(2,128)(2,1)} fusion(f32[64,4,16384]{2,1,0:T(4,128)} %reshape.103, pred[64,4]{1,0:T(8,128)(4,1)S(1)} %iota_compare_fusion, s32[64,4]{1,0:T(8,128)S(1)} %bitcast.50), kind=kOutput, calls=%fused_computation.1 | convolution fusion | flops 102761472 | bytes 20972800 | tf_op jit(solution)/shard_map/rkb,rkx->rbx/dot_general | solution.py:88
  101.5 8.0 %convert_element_type.45 = bf16[64,256,128]{2,1,0:T(8,128)(2,1)} reshape(bf16[64,2,16384]{2,1,0:T(2,128)(2,1)} %convolution_convert_fusion) | data formatting | bytes 8388608 | tf_op jit(solution)/shard_map/convert_element_type | solution.py:90
  109.5 10.7 %all-to-all-start.1 = ((bf16[64,256,128]{2,1,0:T(8,128)(2,1)}), bf16[64,256,128]{2,1,0:T(8,128)(2,1)}, u32[]{:S(2)}, u32[]{:S(2)}) async-start(bf16[64,256,128]{2,1,0:T(8,128)(2,1)} %convert_element_type.45), calls=%async_computation.1 | async-start | bytes 8388608 | tf_op jit(solution)/shard_map/all_to_all | solution.py:32
  120.2 95.8 %all-to-all-done.1 = bf16[64,256,128]{2,1,0:T(8,128)(2,1)} async-done(((bf16[64,256,128]{2,1,0:T(8,128)(2,1)}), bf16[64,256,128]{2,1,0:T(8,128)(2,1)}, u32[]{:S(2)}, u32[]{:S(2)}) %all-to-all-start.1) | async-done | bytes 4194336 | tf_op jit(solution)/shard_map/all_to_all | solution.py:32
  216.0 2.8 %convert_reduce_fusion = f32[256,128]{1,0:T(8,128)S(1)} fusion(bf16[64,256,128]{2,1,0:T(8,128)(2,1)} %all-to-all-done.1), kind=kLoop, calls=%fused_computation.3 | loop fusion | flops 4161536 | bytes 4325376 | tf_op jit(solution)/shard_map/reduce_sum | solution.py:33
  218.8 0.0 copy-done.2
  218.8 0.0 copy-done.3
  218.8 0.2 fusion.13
  219.1 0.6 pad_maximum_fusion
  219.7 4.2 %all-to-all-start.2 = ((bf16[4,64,128]{2,1,0:T(8,128)(2,1)}), bf16[4,64,128]{2,1,0:T(8,128)(2,1)S(1)}, u32[]{:S(2)}, u32[]{:S(2)}) async-start(bf16[4,64,128]{2,1,0:T(8,128)(2,1)} %pad_maximum_fusion), calls=%async_computation.2 | async-start | bytes 131072 | tf_op jit(solution)/shard_map/all_to_all | solution.py:13
  223.9 0.0 copy-done.4
  223.9 4.5 %all-to-all-done.2 = bf16[4,64,128]{2,1,0:T(8,128)(2,1)S(1)} async-done(((bf16[4,64,128]{2,1,0:T(8,128)(2,1)}), bf16[4,64,128]{2,1,0:T(8,128)(2,1)S(1)}, u32[]{:S(2)}, u32[]{:S(2)}) %all-to-all-start.2) | async-done | bytes 65568 | tf_op jit(solution)/shard_map/all_to_all | solution.py:13
  228.4 0.1 fusion.14
  228.5 0.7 fusion.16
  229.2 0.0 copy-done.1
  (14 shorter events, 0.1 us)
Async XLA Ops:
  0.0 15.6 %copy-start = (bf16[20,512,128]{2,1,0:T(8,128)(2,1)S(1)}, bf16[20,512,128]{2,1,0:T(8,128)(2,1)}, u32[]{:S(2)}) copy-start(bf16[20,512,128]{2,1,0:T(8,128)(2,1)} %param.16) | copy-start | bytes 7864324
  1.6 78.2 %all-to-all-start = ((s32[64,1,5]{2,1,0:T(1,128)}), s32[64,1,5]{2,1,0:T(1,128)S(1)}, u32[]{:S(2)}, u32[]{:S(2)}) async-start(s32[64,1,5]{2,1,0:T(1,128)} %bitcast.1), calls=%async_computation | async-start | bytes 65536 | tf_op jit(solution)/shard_map/all_to_all | solution.py:20
  101.5 18.6 %copy-start.5 = (bf16[128]{0:T(256)(128)(2,1)S(1)}, bf16[128]{0:T(256)(128)(2,1)}, u32[]{:S(2)}) copy-start(bf16[128]{0:T(256)(128)(2,1)} %param.18) | copy-start | bytes 772
  101.5 127.7 %copy-start.1 = (bf16[20,512,128]{2,1,0:T(8,128)(2,1)S(1)}, bf16[20,512,128]{2,1,0:T(8,128)(2,1)}, u32[]{:S(2)}) copy-start(bf16[20,512,128]{2,1,0:T(8,128)(2,1)} %param.16) | copy-start | bytes 7864324
  109.5 109.3 %copy-start.2 = (bf16[256,512]{1,0:T(8,128)(2,1)S(1)}, bf16[256,512]{1,0:T(8,128)(2,1)}, u32[]{:S(2)}) copy-start(bf16[256,512]{1,0:T(8,128)(2,1)} %param.10) | copy-start | bytes 786436
  109.5 109.3 %copy-start.3 = (bf16[512,128]{1,0:T(8,128)(2,1)S(1)}, bf16[512,128]{1,0:T(8,128)(2,1)}, u32[]{:S(2)}) copy-start(bf16[512,128]{1,0:T(8,128)(2,1)} %param.17) | copy-start | bytes 393220
  109.5 114.4 %copy-start.4 = (bf16[512]{0:T(512)(128)(2,1)S(1)}, bf16[512]{0:T(512)(128)(2,1)}, u32[]{:S(2)}) copy-start(bf16[512]{0:T(512)(128)(2,1)} %param.19) | copy-start | bytes 3076
  109.5 106.5 %all-to-all-start.1 = ((bf16[64,256,128]{2,1,0:T(8,128)(2,1)}), bf16[64,256,128]{2,1,0:T(8,128)(2,1)}, u32[]{:S(2)}, u32[]{:S(2)}) async-start(bf16[64,256,128]{2,1,0:T(8,128)(2,1)} %convert_element_type.45), calls=%async_computation.1 | async-start | bytes 8388608 | tf_op jit(solution)/shard_map/all_to_all | solution.py:32
  219.7 8.7 %all-to-all-start.2 = ((bf16[4,64,128]{2,1,0:T(8,128)(2,1)}), bf16[4,64,128]{2,1,0:T(8,128)(2,1)S(1)}, u32[]{:S(2)}, u32[]{:S(2)}) async-start(bf16[4,64,128]{2,1,0:T(8,128)(2,1)} %pad_maximum_fusion), calls=%async_computation.2 | async-start | bytes 131072 | tf_op jit(solution)/shard_map/all_to_all | solution.py:13
